TPU v7x, 32 devices: a whole 2x2x4 slice. The times are simulated.
32 devices in a mesh: row: 8 (over y, x, core), col: 4 (over z).
Axes of the slice: x: 2, y: 2, z: 4, core: 2. Of those that a mesh axis runs over, the one named last changes fastest.
Arguments:
- eigvectors: bfloat16 [14336, 256], P(('col', 'row')), may hold values from -0.046875 to 0.046875
- eigvalues: float32 [256], replicated, may hold values from -0.6 to 0.99
- degrees: float32 [14336], P(('col', 'row')), may hold values from 1 to 180
- sketch: bfloat16 [14336, 256], P(('col', 'row')), may hold values from -0.046875 to 0.046875
Outputs:
- embedding: float32 [14336, 256], P(('col', 'row'))
All inputs are finite; a program needn't handle non-finite values.
Results may differ from a plain program's by a relative error of at most 0.0071.
Values may be sent and summed in bfloat16 or wider, within the bound.
A program may use at most 64 MiB of HBM per device.

v0:
```python
import jax
import jax.numpy as jnp
from jax import lax
from jax.sharding import PartitionSpec as P

WINDOW = 10


def spectrum(eigvalues):
    total = jnp.zeros_like(eigvalues)
    powers = jnp.ones_like(eigvalues)
    for counter in range(WINDOW):
        powers = powers * eigvalues
        total = total + powers
    return total / WINDOW


def add_tile(left_rows, volume, running, right_block, sketch_block):
    products = lax.dot_general(
        left_rows, right_block, (((1,), (1,)), ((), ())), preferred_element_type=jnp.float32
    )
    matrix = volume * products
    log_values = jnp.log(jnp.maximum(matrix, 1.0)).astype(jnp.bfloat16)
    return running + jnp.dot(log_values, sketch_block, preferred_element_type=jnp.float32)


def accumulate(left_rows, volume, running, pieces):
    right_piece, sketch_piece = pieces
    piece_rows = right_piece.shape[0]
    right_tiles = right_piece.reshape(piece_rows // 512, 512, right_piece.shape[1])
    sketch_tiles = sketch_piece.reshape(piece_rows // 512, 512, sketch_piece.shape[1])

    def step_tile(current, tiles):
        return (add_tile(left_rows, volume, current, tiles[0], tiles[1]), None)

    running, unused = lax.scan(step_tile, running, (right_tiles, sketch_tiles))
    return running


def local(eigvectors, eigvalues, degrees, sketch):
    right = (eigvectors.astype(jnp.float32) * lax.rsqrt(degrees)[:, None]).astype(jnp.bfloat16)
    volume = lax.psum(jnp.sum(degrees), ("row", "col"))
    spectral = spectrum(eigvalues)
    gathered = lax.all_gather(right, "col", axis=0, tiled=True)
    left_rows = (gathered.astype(jnp.float32) * spectral[None, :]).astype(jnp.bfloat16)
    initial = jnp.zeros((left_rows.shape[0], sketch.shape[1]), jnp.float32)
    partial_sums = accumulate(
        left_rows,
        volume,
        initial,
        (
            lax.all_gather(right, "row", axis=0, tiled=True),
            lax.all_gather(sketch, "row", axis=0, tiled=True),
        ),
    )
    result = lax.psum_scatter(partial_sums, "col", scatter_dimension=0, tiled=True)
    return result


def solution(mesh):
    return jax.shard_map(
        local,
        mesh=mesh,
        in_specs=(P(("col", "row"), None), P(), P(("col", "row")), P(("col", "row"), None)),
        out_specs=P(("col", "row"), None),
        check_vma=False,
    )
```

profile of v0, /device:TPU:0, one launch (start us, length us, event | category | flops | bytes accessed | tf_op | source)
XLA Modules:
  0.0 147.0 jit_solution(4698648812853255453)
XLA Ops:
  6.5 0.0 all-gather.5.cloned.1.call-start
  6.5 0.7 all-gather.5.cloned.1.call-update
  7.3 0.0 all-gather.3.cloned.1.call-start
  7.3 1.4 fusion.15
  8.7 1.8 %multiply_convert_fusion.1 = bf16[448,256]{1,0:T(8,128)(2,1)} fusion(bf16[448,256]{1,0:T(8,128)(2,1)} %param.6, f32[448]{0:T(512)S(1)} %get-tuple-element.71), kind=kLoop, calls=%fused_computation.9 | loop fusion | flops 344064 | bytes 460544 | tf_op jit(solution)/shard_map/convert_element_type | solution.py:41
  10.4 0.0 all-gather.3.cloned.1.call-update
  10.4 0.0 reduce-scatter.2.cloned.1.call-start
  10.5 42.4 %psum.7 = f32[]{:T(128)} all-reduce(f32[]{:T(128)} %get-tuple-element.72), channel_id=1, replica_groups=mesh['row'=8,'col'=4] {'row','col'}, use_global_device_ids=true, to_apply=%region_1.0 | all-reduce | flops 1 | bytes 8 | tf_op jit(solution)/shard_map/psum | solution.py:42
  52.9 0.7 add_multiply_fusion
  53.6 20.1 %all_gather.10 = bf16[1792,256]{1,0:T(8,128)(2,1)S(1)} all-gather(bf16[448,256]{1,0:T(8,128)(2,1)} %multiply_convert_fusion.1), channel_id=1, replica_groups=mesh['row'=8,'col'=4] {'col'}, dimensions={0}, use_global_device_ids=true | all-gather | bytes 1146880 | tf_op jit(solution)/shard_map/all_gather | solution.py:44
  73.7 0.2 multiply_convert_fusion
  73.9 0.0 all-gather.5.cloned.1.call-done
  74.0 0.0 all-gather.3.cloned.1.call-done
  74.0 26.3 %while.11 = (s32[]{:T(128)}, f32[1792,256]{1,0:T(8,128)S(1)}, f32[]{:T(128)}, bf16[7,512,256]{2,1,0:T(8,128)(2,1)}, bf16[1792,256]{1,0:T(8,128)(2,1)S(1)}, /*ind...) while((s32[]{:T(128)}, f32[1792,256]{1,0:T(8,128)S(1)}, f32[]{:T(128)}, ...), condition=%wide.region_3.4_spmd.clone, body=%wide.region_2.3_spmd.clone.sunk | while | flops 943194112 | bytes 5113958 | solution.py:36
  74.0 3.7 %convolution_add_fusion.2 = f32[1792,256]{1,0:T(8,128)S(1)} fusion(f32[1792,256]{1,0:T(8,128)S(1)} %get-tuple-element.119, bf16[1792,256]{1,0:T(8,128)(2,1)S(1)} %get-tuple-element.130, f32[]{:T(128)} %get-tuple-element.128, pred[]{:T(512)S(6)} %compare.3, bf16[7,512,256]{2,1,0:T(8,128)(2,1)} %get-tuple-element.131, s32[]{:T(128)S(6)} %copy.7, ...), kind=kOutput, calls=%fused_computation.1.clone.1 | convolution fusion | flops 943194112 | bytes 5113856 | tf_op jit(solution)/shard_map/while/body/eval_jaxpr/dot_general | solution.py:24
  77.8 3.7 %convolution_add_fusion.2 = f32[1792,256]{1,0:T(8,128)S(1)} fusion(f32[1792,256]{1,0:T(8,128)S(1)} %get-tuple-element.119, bf16[1792,256]{1,0:T(8,128)(2,1)S(1)} %get-tuple-element.130, f32[]{:T(128)} %get-tuple-element.128, pred[]{:T(512)S(6)} %compare.3, bf16[7,512,256]{2,1,0:T(8,128)(2,1)} %get-tuple-element.131, s32[]{:T(128)S(6)} %copy.7, ...), kind=kOutput, calls=%fused_computation.1.clone.1 | convolution fusion | flops 943194112 | bytes 5113856 | tf_op jit(solution)/shard_map/while/body/eval_jaxpr/dot_general | solution.py:24
  81.5 3.7 %convolution_add_fusion.2 = f32[1792,256]{1,0:T(8,128)S(1)} fusion(f32[1792,256]{1,0:T(8,128)S(1)} %get-tuple-element.119, bf16[1792,256]{1,0:T(8,128)(2,1)S(1)} %get-tuple-element.130, f32[]{:T(128)} %get-tuple-element.128, pred[]{:T(512)S(6)} %compare.3, bf16[7,512,256]{2,1,0:T(8,128)(2,1)} %get-tuple-element.131, s32[]{:T(128)S(6)} %copy.7, ...), kind=kOutput, calls=%fused_computation.1.clone.1 | convolution fusion | flops 943194112 | bytes 5113856 | tf_op jit(solution)/shard_map/while/body/eval_jaxpr/dot_general | solution.py:24
  85.3 3.7 %convolution_add_fusion.2 = f32[1792,256]{1,0:T(8,128)S(1)} fusion(f32[1792,256]{1,0:T(8,128)S(1)} %get-tuple-element.119, bf16[1792,256]{1,0:T(8,128)(2,1)S(1)} %get-tuple-element.130, f32[]{:T(128)} %get-tuple-element.128, pred[]{:T(512)S(6)} %compare.3, bf16[7,512,256]{2,1,0:T(8,128)(2,1)} %get-tuple-element.131, s32[]{:T(128)S(6)} %copy.7, ...), kind=kOutput, calls=%fused_computation.1.clone.1 | convolution fusion | flops 943194112 | bytes 5113856 | tf_op jit(solution)/shard_map/while/body/eval_jaxpr/dot_general | solution.py:24
  89.0 3.7 %convolution_add_fusion.2 = f32[1792,256]{1,0:T(8,128)S(1)} fusion(f32[1792,256]{1,0:T(8,128)S(1)} %get-tuple-element.119, bf16[1792,256]{1,0:T(8,128)(2,1)S(1)} %get-tuple-element.130, f32[]{:T(128)} %get-tuple-element.128, pred[]{:T(512)S(6)} %compare.3, bf16[7,512,256]{2,1,0:T(8,128)(2,1)} %get-tuple-element.131, s32[]{:T(128)S(6)} %copy.7, ...), kind=kOutput, calls=%fused_computation.1.clone.1 | convolution fusion | flops 943194112 | bytes 5113856 | tf_op jit(solution)/shard_map/while/body/eval_jaxpr/dot_general | solution.py:24
  92.8 3.7 %convolution_add_fusion.2 = f32[1792,256]{1,0:T(8,128)S(1)} fusion(f32[1792,256]{1,0:T(8,128)S(1)} %get-tuple-element.119, bf16[1792,256]{1,0:T(8,128)(2,1)S(1)} %get-tuple-element.130, f32[]{:T(128)} %get-tuple-element.128, pred[]{:T(512)S(6)} %compare.3, bf16[7,512,256]{2,1,0:T(8,128)(2,1)} %get-tuple-element.131, s32[]{:T(128)S(6)} %copy.7, ...), kind=kOutput, calls=%fused_computation.1.clone.1 | convolution fusion | flops 943194112 | bytes 5113856 | tf_op jit(solution)/shard_map/while/body/eval_jaxpr/dot_general | solution.py:24
  96.6 3.7 %convolution_add_fusion.2 = f32[1792,256]{1,0:T(8,128)S(1)} fusion(f32[1792,256]{1,0:T(8,128)S(1)} %get-tuple-element.119, bf16[1792,256]{1,0:T(8,128)(2,1)S(1)} %get-tuple-element.130, f32[]{:T(128)} %get-tuple-element.128, pred[]{:T(512)S(6)} %compare.3, bf16[7,512,256]{2,1,0:T(8,128)(2,1)} %get-tuple-element.131, s32[]{:T(128)S(6)} %copy.7, ...), kind=kOutput, calls=%fused_computation.1.clone.1 | convolution fusion | flops 943194112 | bytes 5113856 | tf_op jit(solution)/shard_map/while/body/eval_jaxpr/dot_general | solution.py:24
  100.3 1.2 copy-done
  101.6 0.0 reduce-scatter.2.cloned.1.call-update
  101.6 38.9 %reduce-scatter.2.cloned.1.call-done = f32[448,256]{1,0:T(8,128)} async-done(((f32[1792,256]{1,0:T(8,128)}), f32[448,256]{1,0:T(8,128)}) %reduce-scatter.2.cloned.1.call-update) | async-done | bytes 458768 | tf_op jit(solution)/shard_map/reduce_scatter | solution.py:56
  (2 shorter events, 0.0 us)
Async XLA Ops:
  6.5 67.4 %all-gather.5.cloned.1.call-start = ((), (), s32[]{:S(2)}) async-start(), calls=%async_computation.2 | async-start | bytes 2064384 | tf_op jit(solution)/shard_map/all_gather | solution.py:53
  7.3 66.7 %all-gather.3.cloned.1.call-start = ((), (), s32[]{:S(2)}) async-start(), calls=%async_computation.1 | async-start | bytes 2064384 | tf_op jit(solution)/shard_map/all_gather | solution.py:52
  10.4 130.0 %reduce-scatter.2.cloned.1.call-start = ((), (), s32[]{:S(2)}) async-start(), calls=%async_computation.3 | async-start | bytes 2293760 | tf_op jit(solution)/shard_map/reduce_scatter | solution.py:56
  100.3 1.3 copy-start
Sparse Core Ops, SparseCore 0:
  9.2 29.5 all-gather.4
  40.6 26.8 all-gather.2
  101.7 38.7 reduce-scatter.1
where the time goes:
time: 147 us
  blocking collectives  62.5 us (43%)
  waiting for transfers between devices  39.7 us (27%)
  matrix products  26.2 us (18%)
  between operations  13.1 us (9%)
  other arithmetic  4.01 us (3%)
    psum x1, blocking collectives, local(): volume = lax.psum(jnp.sum(degrees), ('row', 'col'))  42.4 us
    reduce_scatter x1, waiting for transfers between devices, local(): lax.psum_scatter(partial_sums, 'col', scatter_dimension=0, tiled=True)  38.9 us
    dot_general x7, matrix products, add_tile(): jnp.dot(log_values, sketch_block, preferred_element_type=jnp.float32)  26.2 us
    all_gather x1, blocking collectives, local(): gathered = lax.all_gather(right, 'col', axis=0, tiled=True)  20.1 us
  transfers between devices with their start and end apart: 3, of which 1 were waited for; matrix products, arithmetic and copies ran while one was open for 3% of the time, Pallas kernels for 0%

commit v1 on v0

v1 whole, which is shorter than its diff:
```python
import functools

import jax
import jax.numpy as jnp
from jax import lax
from jax.experimental import pallas as pl
from jax.experimental.pallas import tpu as pltpu
from jax.sharding import PartitionSpec as P

WINDOW = 10
MESH = pl.DeviceIdType.MESH


def spectrum(eigvalues):
    total = jnp.zeros_like(eigvalues)
    powers = jnp.ones_like(eigvalues)
    for counter in range(WINDOW):
        powers = powers * eigvalues
        total = total + powers
    return total / WINDOW


def kernel(nrow, ncol, right_ref, sketch_ref, deg_ref, eig_ref, out_ref,
           cright, csketch, rright, left, acc, sendbuf, recvbuf, dsum, drow, dpart, dcol,
           c_send, c_recv, z_send, z_recv, v_send, v_recv, w_send, w_recv, p_send, p_recv):
    r = lax.axis_index("row")
    c = lax.axis_index("col")
    chips = nrow // 2
    core = lax.rem(r, 2)
    chip = r // 2
    partner = (r + 1 - 2 * core, c)

    def row_peer(j):
        return (lax.rem(r + j, nrow), c)

    def col_peer(o):
        return (r, lax.rem(c + o, ncol))

    barrier = pltpu.get_barrier_semaphore()
    for j in range(1, nrow):
        pl.semaphore_signal(barrier, inc=1, device_id=row_peer(j), device_id_type=MESH)
    for o in range(1, ncol):
        pl.semaphore_signal(barrier, inc=1, device_id=col_peer(o), device_id_type=MESH)
    dsum[...] = jnp.full(dsum.shape, jnp.sum(deg_ref[...]), jnp.float32)
    pl.semaphore_wait(barrier, nrow + ncol - 2)

    def remote(src, dst, ssem, rsem, dev):
        return pltpu.make_async_remote_copy(
            src_ref=src, dst_ref=dst, send_sem=ssem, recv_sem=rsem,
            device_id=dev, device_id_type=MESH)

    bufs = (cright, csketch)
    owns = (right_ref, sketch_ref)
    started = []

    def start(copy):
        copy.start()
        started.append(copy)

    def c_copy(kind, src_slot, dst_slot, dev):
        src = owns[kind] if src_slot == 0 else bufs[kind].at[src_slot]
        return remote(src, bufs[kind].at[dst_slot], c_send.at[kind, dst_slot],
                      c_recv.at[kind, dst_slot], dev)

    def c_wait(kind, slot):
        c_copy(kind, 0, slot, partner).wait_recv()

    for j in range(1, nrow):
        start(remote(dsum, drow.at[j], v_send.at[j], v_recv.at[j], row_peer(j)))

    relay = chips == 4
    if relay:
        x_peer = chip + 1 - 2 * lax.rem(chip, 2)
        y_peer = lax.rem(chip + 2, 4)
        first = x_peer * (1 - core) + y_peer * core
        second = y_peer * (1 - core) + x_peer * core
        first = (first * 2 + core, c)
        second = (second * 2 + core, c)
        targets = [(1, first), (2, second)]
    else:
        targets = [(o, (lax.rem(chip + o, chips) * 2 + core, c)) for o in range(1, chips)]

    order = sorted(range(1, ncol), key=lambda o: -min(o, ncol - o))
    for kind in (0, 1):
        start(c_copy(kind, 0, 1, partner))
        for o, dev in targets:
            start(c_copy(kind, 0, 2 * o, dev))
        if kind == 0:
            for o in reversed(order):
                start(remote(right_ref, rright.at[o], z_send.at[o], z_recv.at[o], col_peer(o)))

    total = dsum[...]
    for j in range(1, nrow):
        remote(dsum, drow.at[j], v_send.at[j], v_recv.at[j], row_peer(j)).wait_recv()
        total = total + drow[j]
    dpart[...] = total
    spectral = spectrum(eig_ref[...])
    acc[...] = jnp.zeros_like(acc)
    left[0] = (right_ref[...].astype(jnp.float32) * spectral).astype(jnp.bfloat16)
    for o in range(1, ncol):
        start(remote(dpart, dcol.at[o], w_send.at[o], w_recv.at[o], col_peer(o)))
    for o in range(1, ncol):
        remote(dpart, dcol.at[o], w_send.at[o], w_recv.at[o], col_peer(o)).wait_recv()
        total = total + dcol[o]
    volume = total[0:1, 0:1]

    def tile(o, slot):
        cr = right_ref if slot == 0 else cright.at[slot]
        cs = sketch_ref if slot == 0 else csketch.at[slot]
        products = lax.dot_general(left[o], cr[...], (((1,), (1,)), ((), ())),
                                   preferred_element_type=jnp.float32)
        logs = jnp.log(jnp.maximum(volume * products, 1.0)).astype(jnp.bfloat16)
        acc[o] += jnp.dot(logs, cs[...], preferred_element_type=jnp.float32)

    def row_arrive(o):
        remote(right_ref, rright.at[o], z_send.at[o], z_recv.at[o], col_peer(o)).wait_recv()
        left[o] = (rright[o].astype(jnp.float32) * spectral).astype(jnp.bfloat16)

    def tiles(o, slots):
        for slot in slots:
            tile(o, slot)

    def many(lo, hi, slots):
        def step(o, carry):
            tiles(o, slots)
            return carry
        lax.fori_loop(lo, hi, step, 0)

    def c_arrive(kind, o):
        c_wait(kind, 2 * o)
        start(c_copy(kind, 2 * o, 2 * o + 1, partner))
        if relay and o == 1:
            start(c_copy(kind, 2, 6, second))

    tiles(0, [0])
    c_wait(0, 1)
    c_wait(1, 1)
    tiles(0, [1])
    c_arrive(0, 1)
    c_arrive(0, 2)
    for o in range(1, ncol):
        row_arrive(o)
    many(1, ncol, [0, 1])
    c_arrive(1, 1)
    c_arrive(1, 2)
    c_wait(0, 3)
    c_wait(1, 3)
    c_wait(0, 5)
    c_wait(1, 5)
    if relay:
        many(0, ncol, [2, 3, 4, 5])
        rest = [6, 7]
        c_arrive(0, 3)
        c_arrive(1, 3)
    else:
        many(0, ncol, [2, 3, 4, 5])
        rest = []
        for o in range(3, chips):
            c_arrive(0, o)
            c_arrive(1, o)
            rest += [2 * o, 2 * o + 1]
    for slot in rest[1::2]:
        c_wait(0, slot)
        c_wait(1, slot)

    def finish(o):
        if relay:
            tiles(o, rest)
        else:
            def step(slot, carry):
                products = lax.dot_general(left[o], cright[slot], (((1,), (1,)), ((), ())),
                                           preferred_element_type=jnp.float32)
                logs = jnp.log(jnp.maximum(volume * products, 1.0)).astype(jnp.bfloat16)
                acc[o] += jnp.dot(logs, csketch[slot], preferred_element_type=jnp.float32)
                return carry
            lax.fori_loop(6, 2 * chips, step, 0)

    def p_copy(o):
        return remote(sendbuf.at[o], recvbuf.at[o], p_send.at[o], p_recv.at[o], col_peer(o))

    for o in order:
        finish(o)
        sendbuf[ncol - o] = acc[o].astype(jnp.bfloat16)
        start(p_copy(ncol - o))
    finish(0)
    for o in reversed(order):
        p_copy(o).wait_recv()
        acc[0] += recvbuf[o].astype(jnp.float32)
    out_ref[...] = acc[0]
    for copy in started:
        copy.wait_send()


def local(nrow, ncol, eigvectors, eigvalues, degrees, sketch):
    rows, width = eigvectors.shape
    cols = sketch.shape[1]
    right = (eigvectors.astype(jnp.float32) * lax.rsqrt(degrees)[:, None]).astype(jnp.bfloat16)
    vmem = pl.BlockSpec(memory_space=pltpu.VMEM)
    dma = pltpu.SemaphoreType.DMA
    return pl.pallas_call(
        functools.partial(kernel, nrow, ncol),
        out_shape=jax.ShapeDtypeStruct((rows, cols), jnp.float32),
        in_specs=[vmem] * 4,
        out_specs=vmem,
        scratch_shapes=[
            pltpu.VMEM((nrow, rows, width), jnp.bfloat16),
            pltpu.VMEM((nrow, rows, cols), jnp.bfloat16),
            pltpu.VMEM((ncol, rows, width), jnp.bfloat16),
            pltpu.VMEM((ncol, rows, width), jnp.bfloat16),
            pltpu.VMEM((ncol, rows, cols), jnp.float32),
            pltpu.VMEM((ncol, rows, cols), jnp.bfloat16),
            pltpu.VMEM((ncol, rows, cols), jnp.bfloat16),
            pltpu.VMEM((8, 128), jnp.float32),
            pltpu.VMEM((nrow, 8, 128), jnp.float32),
            pltpu.VMEM((8, 128), jnp.float32),
            pltpu.VMEM((ncol, 8, 128), jnp.float32),
            dma((2, nrow)), dma((2, nrow)),
            dma((ncol,)), dma((ncol,)),
            dma((nrow,)), dma((nrow,)),
            dma((ncol,)), dma((ncol,)),
            dma((ncol,)), dma((ncol,)),
        ],
        compiler_params=pltpu.CompilerParams(
            collective_id=0, has_side_effects=True, vmem_limit_bytes=56 * 1024 * 1024),
    )(right, sketch, degrees.reshape(1, rows), eigvalues.reshape(1, width))


def solution(mesh):
    return jax.shard_map(
        functools.partial(local, mesh.shape["row"], mesh.shape["col"]),
        mesh=mesh,
        in_specs=(P(("col", "row"), None), P(), P(("col", "row")), P(("col", "row"), None)),
        out_specs=P(("col", "row"), None),
        check_vma=False,
    )
```

time: 147 us -> 64.3 us (0.44)
  the two profiles are of different devices: /device:TPU:0 before, /device:TPU:16 now
where the time goes in v1:
time: 64.3 us; the launch traced here: 64.1 us
  Pallas kernels  59.8 us (93%)
  local copies, waits for them, and re-layouts  2.5 us (4%)
  other arithmetic  1.76 us (3%)
    pallas_call x1, Pallas kernels, local(): pl.pallas_call(functools.partial(kernel, nrow, ncol), out_shape=jax.Shape...  59.8 us
    unnamed x3, local copies, waits for them, and re-layouts  2.5 us
    convert_element_type x1, other arithmetic, local(): (eigvectors.astype(jnp.float32) * lax.rsqrt(degrees)[:, None]).astype(jnp...  1.76 us

profile of v1, /device:TPU:16, one launch (start us, length us, event | category | flops | bytes accessed | tf_op | source)
XLA Modules:
  0.0 64.1 jit_solution(14145826858347074884)
XLA Ops:
  0.0 0.0 copy-start
  0.0 0.7 %copy-done = f32[448]{0:T(512)S(1)} copy-done((f32[448]{0:T(512)S(1)}, f32[448]{0:T(512)}, u32[]{:S(2)}) %copy-start) | copy-done | bytes 1816
  0.7 1.8 %multiply_convert_fusion.right_ref = bf16[448,256]{1,0:T(8,128)(2,1)} fusion(bf16[448,256]{1,0:T(8,128)(2,1)} %param.4, f32[448]{0:T(512)S(1)} %rsqrt.3), kind=kLoop, calls=%fused_computation | loop fusion | flops 344064 | bytes 460544 | tf_op jit(solution)/shard_map/convert_element_type | solution.py:197
  2.4 59.8 %shard_map.46 = f32[448,256]{1,0:T(8,128)} custom-call(bf16[448,256]{1,0:T(8,128)(2,1)} %multiply_convert_fusion.right_ref, bf16[448,256]{1,0:T(8,128)(2,1)} %sketch_ref.1, f32[1,448]{1,0:T(1,128)} %bitcast.2, f32[1,256]{1,0:T(1,128)} %bitcast.3), custom_call_target="tpu_custom_call" | custom-call | tf_op jit(solution)/shard_map/pallas_call | solution.py:200
  62.3 1.8 %copy.6 = f32[448,256]{1,0:T(8,128)} copy(f32[448,256]{1,0:T(8,128)} %shard_map.46) | data formatting | bytes 917504
  (1 shorter events, 0.0 us)
Async XLA Ops:
  0.0 0.7 %copy-start = (f32[448]{0:T(512)S(1)}, f32[448]{0:T(512)}, u32[]{:S(2)}) copy-start(f32[448]{0:T(512)} %param.6) | copy-start | bytes 5380

commit v2 on v1

v2 whole, which is shorter than its diff:
```python
import functools

import jax
import jax.numpy as jnp
from jax import lax
from jax.experimental import pallas as pl
from jax.experimental.pallas import tpu as pltpu
from jax.sharding import PartitionSpec as P

WINDOW = 10
MESH = pl.DeviceIdType.MESH


def spectrum(eigvalues):
    total = jnp.zeros_like(eigvalues)
    powers = jnp.ones_like(eigvalues)
    for counter in range(WINDOW):
        powers = powers * eigvalues
        total = total + powers
    return total / WINDOW


def kernel(nrow, ncol, right_ref, sketch_ref, deg_ref, eig_ref, out_ref,
           cright, csketch, rright, left, acc, sendbuf, recvbuf, dsum, dall,
           c_send, c_recv, z_send, z_recv, v_send, v_recv, p_send, p_recv):
    r = lax.axis_index("row")
    c = lax.axis_index("col")
    chips = nrow // 2
    core = lax.rem(r, 2)
    chip = r // 2
    partner = (r + 1 - 2 * core, c)

    rows = right_ref.shape[0]
    half = rows // 32 * 16
    everyone = nrow * ncol
    me = c * nrow + r

    def device(j):
        other = lax.rem(me + j, everyone)
        return (lax.rem(other, nrow), other // nrow)

    barrier = pltpu.get_barrier_semaphore()

    def greet(j, carry):
        pl.semaphore_signal(barrier, inc=1, device_id=device(j), device_id_type=MESH)
        return carry
    lax.fori_loop(1, everyone, greet, 0)
    dsum[...] = jnp.full(dsum.shape, jnp.sum(deg_ref[...]), jnp.float32)
    pl.semaphore_wait(barrier, everyone - 1)

    def remote(src, dst, ssem, rsem, dev):
        return pltpu.make_async_remote_copy(
            src_ref=src, dst_ref=dst, send_sem=ssem, recv_sem=rsem,
            device_id=dev, device_id_type=MESH)

    bufs = (cright, csketch)
    owns = (right_ref, sketch_ref)
    started = []

    def start(copy):
        copy.start()
        started.append(copy)

    def c_copy(kind, src_slot, dst_slot, dev):
        src = owns[kind] if src_slot == 0 else bufs[kind].at[src_slot]
        return remote(src, bufs[kind].at[dst_slot], c_send.at[kind, dst_slot],
                      c_recv.at[kind, dst_slot], dev)

    def c_wait(kind, slot):
        c_copy(kind, 0, slot, partner).wait_recv()

    def v_copy(j):
        return remote(dsum, dall.at[j], v_send.at[j], v_recv.at[j], device(j))

    def v_start(j, carry):
        v_copy(j).start()
        return carry
    lax.fori_loop(1, everyone, v_start, 0)
    dall[0] = dsum[...]

    relay = chips == 4
    if relay:
        x_peer = chip + 1 - 2 * lax.rem(chip, 2)
        y_peer = lax.rem(chip + 2, 4)
        first = x_peer * (1 - core) + y_peer * core
        second = y_peer * (1 - core) + x_peer * core
        first = (first * 2 + core, c)
        second = (second * 2 + core, c)
        targets = [(1, first), (2, second)]
    else:
        targets = [(o, (lax.rem(chip + o, chips) * 2 + core, c)) for o in range(1, chips)]

    line = ncol == 4
    if line:
        inner = lax.rem((c + 1) // 2, 2)
        way = 1 - 2 * (c // 2)
    else:
        inner, way = 1, 1

    def at(i):
        return lax.rem(c + i * way + ncol, ncol)

    def pick(end_i, inner_i):
        return at(end_i * (1 - inner) + inner_i * inner) if line else at(inner_i)

    def when_inner(fn):
        if line:
            pl.when(inner == 1)(fn)
        else:
            fn()

    def when_end(fn):
        if line:
            pl.when(inner == 0)(fn)

    halves = (pl.ds(0, half), pl.ds(half, rows - half))

    def z_copies(i):
        return [remote(right_ref.at[h], rright.at[c, h], z_send.at[n, i], z_recv.at[n, c], (r, at(i)))
                for n, h in enumerate(halves)]

    def z_half(n, src):
        h = halves[n]
        remote(right_ref.at[h], rright.at[src, h], z_send.at[n, 0], z_recv.at[n, src], (r, src)).wait_recv()

    def z_wait(src):
        z_half(0, src)
        z_half(1, src)

    def z_relay(n):
        far, h = at(2), halves[n]
        return remote(rright.at[far, h], rright.at[far, h], z_send.at[n, ncol], z_recv.at[n, far], (r, at(3)))

    def z_start(i):
        for copy in z_copies(i):
            copy.start()

    if line:
        z_start(2)
        z_start(1)
        when_inner(lambda: z_start(3))
    else:
        for i in range(1, ncol):
            z_start(i)
    for kind in (0, 1):
        start(c_copy(kind, 0, 1, partner))
        for o, dev in targets:
            start(c_copy(kind, 0, 2 * o, dev))

    spectral = spectrum(eig_ref[...])
    acc[...] = jnp.zeros_like(acc)
    cright[0] = right_ref[...]
    csketch[0] = sketch_ref[...]
    left[c] = (right_ref[...].astype(jnp.float32) * spectral).astype(jnp.bfloat16)

    def v_wait(j, carry):
        v_copy(j).wait_recv()
        return carry
    lax.fori_loop(1, everyone, v_wait, 0)
    volume = jnp.sum(dall[...], axis=0)[0:1, 0:1]

    def tiles(o, lo, hi):
        def step(slot, carry):
            products = lax.dot_general(left[o], cright[slot], (((1,), (1,)), ((), ())),
                                       preferred_element_type=jnp.float32)
            logs = jnp.log(jnp.maximum(volume * products, 1.0)).astype(jnp.bfloat16)
            acc[o] += jnp.dot(logs, csketch[slot], preferred_element_type=jnp.float32)
            return carry
        lax.fori_loop(lo, hi, step, 0)

    def row_scale(src):
        left[src] = (rright[src].astype(jnp.float32) * spectral).astype(jnp.bfloat16)

    def c_arrive(kind, o):
        c_wait(kind, 2 * o)
        start(c_copy(kind, 2 * o, 2 * o + 1, partner))
        if relay and o == 1:
            start(c_copy(kind, 2, 6, second))

    tiles(c, 0, 1)
    c_wait(0, 1)
    c_wait(1, 1)
    tiles(c, 1, 2)
    early = min(chips, 3)
    for o in range(1, early):
        c_arrive(0, o)
    def relay_row(n):
        z_half(n, at(2))
        z_relay(n).start()

    if line:
        when_inner(lambda: relay_row(0))
    first_row = pick(1, 3) if line else at(1)
    z_wait(first_row)
    row_scale(first_row)
    tiles(first_row, 0, 2)
    if line:
        when_inner(lambda: relay_row(1))
    for o in range(1, early):
        c_arrive(1, o)
    for o in range(1, early):
        c_wait(0, 2 * o + 1)
        c_wait(1, 2 * o + 1)
    tiles(c, 2, 2 * early)
    for o in range(early, chips):
        c_arrive(0, o)
    tiles(first_row, 2, 2 * early)
    if line:
        second_row, third_row = at(2), pick(3, 1)
        when_end(lambda: z_wait(second_row))
        row_scale(second_row)
        tiles(second_row, 0, 2 * early)
    for o in range(early, chips):
        c_arrive(1, o)
    if line:
        z_wait(third_row)
        row_scale(third_row)
        tiles(third_row, 0, 2 * early)
    else:
        for i in range(2, ncol):
            z_wait(at(i))
            row_scale(at(i))

        def other(i, carry):
            tiles(at(i), 0, 2 * early)
            return carry
        lax.fori_loop(2, ncol, other, 0)
    for o in range(early, chips):
        c_wait(0, 2 * o + 1)
        c_wait(1, 2 * o + 1)

    def p_copy(step, dst, slot):
        return remote(sendbuf.at[step], recvbuf.at[slot], p_send.at[step], p_recv.at[slot], (r, dst))

    def p_wait(src):
        p_copy(0, src, src).wait_recv()

    def finish(o):
        tiles(o, 2 * early, 2 * chips)

    if line:
        steps = [(pick(3, 1), at(1), ncol * (1 - inner) + c * inner), (pick(2, 3), pick(2, 3), c)]
        for step, (o, dst, slot) in enumerate(steps):
            finish(o)
            sendbuf[step] = acc[o].astype(jnp.bfloat16)
            start(p_copy(step, dst, slot))
        last = pick(1, 2)
        finish(last)

        def send_last():
            sendbuf[2] = acc[last].astype(jnp.bfloat16)
            p_copy(2, last, c).start()
        when_end(send_last)
        finish(c)

        def send_merged():
            p_copy(0, c, ncol).wait_recv()
            acc[last] += recvbuf[ncol].astype(jnp.float32)
            send_last()
        when_inner(send_merged)
        started.append(p_copy(2, last, c))
        p_wait(at(1))
        acc[c] += recvbuf[at(1)].astype(jnp.float32)

        def third():
            p_wait(at(3))
            acc[c] += recvbuf[at(3)].astype(jnp.float32)
        when_inner(third)
        p_wait(at(2))
        out_ref[...] = acc[c] + recvbuf[at(2)].astype(jnp.float32)

        def drain():
            for copy in z_copies(3) + [z_relay(0), z_relay(1)]:
                copy.wait_send()
        when_inner(drain)
    else:
        for i in range(1, ncol):
            finish(at(i))
            sendbuf[i] = acc[at(i)].astype(jnp.bfloat16)
            start(p_copy(i, at(i), c))
        finish(c)
        for i in range(1, ncol):
            p_wait(at(i))
            acc[c] += recvbuf[at(i)].astype(jnp.float32)
        out_ref[...] = acc[c]
    for i in range(1, 3 if line else ncol):
        started.extend(z_copies(i))
    for copy in started:
        copy.wait_send()

    def v_drain(j, carry):
        v_copy(j).wait_send()
        return carry
    lax.fori_loop(1, everyone, v_drain, 0)


def local(nrow, ncol, eigvectors, eigvalues, degrees, sketch):
    rows, width = eigvectors.shape
    cols = sketch.shape[1]
    right = (eigvectors.astype(jnp.float32) * lax.rsqrt(degrees)[:, None]).astype(jnp.bfloat16)
    vmem = pl.BlockSpec(memory_space=pltpu.VMEM)
    dma = pltpu.SemaphoreType.DMA
    return pl.pallas_call(
        functools.partial(kernel, nrow, ncol),
        out_shape=jax.ShapeDtypeStruct((rows, cols), jnp.float32),
        in_specs=[vmem] * 4,
        out_specs=vmem,
        scratch_shapes=[
            pltpu.VMEM((nrow, rows, width), jnp.bfloat16),
            pltpu.VMEM((nrow, rows, cols), jnp.bfloat16),
            pltpu.VMEM((ncol, rows, width), jnp.bfloat16),
            pltpu.VMEM((ncol, rows, width), jnp.bfloat16),
            pltpu.VMEM((ncol, rows, cols), jnp.float32),
            pltpu.VMEM((ncol, rows, cols), jnp.bfloat16),
            pltpu.VMEM((ncol + 1, rows, cols), jnp.bfloat16),
            pltpu.VMEM((1, 128), jnp.float32),
            pltpu.VMEM((nrow * ncol, 1, 128), jnp.float32),
            dma((2, nrow)), dma((2, nrow)),
            dma((2, ncol + 1)), dma((2, ncol)),
            dma((nrow * ncol,)), dma((nrow * ncol,)),
            dma((ncol,)), dma((ncol + 1,)),
        ],
        compiler_params=pltpu.CompilerParams(
            collective_id=0, has_side_effects=True, vmem_limit_bytes=56 * 1024 * 1024),
    )(right, sketch, degrees.reshape(1, rows), eigvalues.reshape(1, width))


def solution(mesh):
    return jax.shard_map(
        functools.partial(local, mesh.shape["row"], mesh.shape["col"]),
        mesh=mesh,
        in_specs=(P(("col", "row"), None), P(), P(("col", "row")), P(("col", "row"), None)),
        out_specs=P(("col", "row"), None),
        check_vma=False,
    )
```

time: 64.3 us -> 55.4 us (0.86)
  the two profiles are of different devices: /device:TPU:16 before, /device:TPU:0 now
where the time goes in v2:
time: 55.4 us; the launch traced here: 55.2 us
  Pallas kernels  50.9 us (92%)
  local copies, waits for them, and re-layouts  2.5 us (5%)
  other arithmetic  1.76 us (3%)
    pallas_call x1, Pallas kernels, local(): pl.pallas_call(functools.partial(kernel, nrow, ncol), out_shape=jax.Shape...  50.9 us
    unnamed x3, local copies, waits for them, and re-layouts  2.5 us
    convert_element_type x1, other arithmetic, local(): (eigvectors.astype(jnp.float32) * lax.rsqrt(degrees)[:, None]).astype(jnp...  1.76 us

profile of v2, /device:TPU:0, one launch (start us, length us, event | category | flops | bytes accessed | tf_op | source)
XLA Modules:
  0.0 55.2 jit_solution(11645636295139403969)
XLA Ops:
  0.0 0.0 copy-start
  0.0 0.7 %copy-done = f32[448]{0:T(512)S(1)} copy-done((f32[448]{0:T(512)S(1)}, f32[448]{0:T(512)}, u32[]{:S(2)}) %copy-start) | copy-done | bytes 1816
  0.7 1.8 %multiply_convert_fusion.right_ref = bf16[448,256]{1,0:T(8,128)(2,1)} fusion(bf16[448,256]{1,0:T(8,128)(2,1)} %param.4, f32[448]{0:T(512)S(1)} %rsqrt.3), kind=kLoop, calls=%fused_computation | loop fusion | flops 344064 | bytes 460544 | tf_op jit(solution)/shard_map/convert_element_type | solution.py:300
  2.4 50.9 %shard_map.46 = f32[448,256]{1,0:T(8,128)} custom-call(bf16[448,256]{1,0:T(8,128)(2,1)} %multiply_convert_fusion.right_ref, bf16[448,256]{1,0:T(8,128)(2,1)} %sketch_ref.1, f32[1,448]{1,0:T(1,128)} %bitcast.2, f32[1,256]{1,0:T(1,128)} %bitcast.3), custom_call_target="tpu_custom_call" | custom-call | tf_op jit(solution)/shard_map/pallas_call | solution.py:303
  53.4 1.8 %copy.6 = f32[448,256]{1,0:T(8,128)} copy(f32[448,256]{1,0:T(8,128)} %shard_map.46) | data formatting | bytes 917504
  (1 shorter events, 0.0 us)
Async XLA Ops:
  0.0 0.7 %copy-start = (f32[448]{0:T(512)S(1)}, f32[448]{0:T(512)}, u32[]{:S(2)}) copy-start(f32[448]{0:T(512)} %param.6) | copy-start | bytes 5380

commit v3 on v2

--- a/solution.py
+++ b/solution.py
@@ -201,7 +201,6 @@
     for o in range(1, early):
         c_wait(0, 2 * o + 1)
         c_wait(1, 2 * o + 1)
-    tiles(c, 2, 2 * early)
     for o in range(early, chips):
         c_arrive(0, o)
     tiles(first_row, 2, 2 * early)
@@ -209,7 +208,6 @@
         second_row, third_row = at(2), pick(3, 1)
         when_end(lambda: z_wait(second_row))
         row_scale(second_row)
-        tiles(second_row, 0, 2 * early)
     for o in range(early, chips):
         c_arrive(1, o)
     if line:
@@ -244,6 +242,8 @@
             finish(o)
             sendbuf[step] = acc[o].astype(jnp.bfloat16)
             start(p_copy(step, dst, slot))
+            if step == 0:
+                tiles(second_row, 0, 2 * early)
         last = pick(1, 2)
         finish(last)
 
@@ -251,7 +251,7 @@
             sendbuf[2] = acc[last].astype(jnp.bfloat16)
             p_copy(2, last, c).start()
         when_end(send_last)
-        finish(c)
+        tiles(c, 2, 2 * chips)
 
         def send_merged():
             p_copy(0, c, ncol).wait_recv()
@@ -278,7 +278,7 @@
             finish(at(i))
             sendbuf[i] = acc[at(i)].astype(jnp.bfloat16)
             start(p_copy(i, at(i), c))
-        finish(c)
+        tiles(c, 2, 2 * chips)
         for i in range(1, ncol):
             p_wait(at(i))
             acc[c] += recvbuf[at(i)].astype(jnp.float32)

time: 55.4 us -> 52.1 us (0.940)
  Pallas kernels: 50.9 us -> 47.6 us
    pallas_call x1, Pallas kernels: 50.9 us -> 47.6 us  [local(): pl.pallas_call(functools.partial(kernel, nrow, ncol), out_shape=jax.Shape...]
where the time goes in v3:
time: 52.1 us; the launch traced here: 51.9 us
  Pallas kernels  47.6 us (91%)
  local copies, waits for them, and re-layouts  2.5 us (5%)
  other arithmetic  1.76 us (3%)
    pallas_call x1, Pallas kernels, local(): pl.pallas_call(functools.partial(kernel, nrow, ncol), out_shape=jax.Shape...  47.6 us
    unnamed x3, local copies, waits for them, and re-layouts  2.5 us
    convert_element_type x1, other arithmetic, local(): (eigvectors.astype(jnp.float32) * lax.rsqrt(degrees)[:, None]).astype(jnp...  1.76 us

profile of v3, /device:TPU:0, one launch (start us, length us, event | category | flops | bytes accessed | tf_op | source)
XLA Modules:
  0.0 51.9 jit_solution(16745623763965992869)
XLA Ops:
  0.0 0.0 copy-start
  0.0 0.7 %copy-done = f32[448]{0:T(512)S(1)} copy-done((f32[448]{0:T(512)S(1)}, f32[448]{0:T(512)}, u32[]{:S(2)}) %copy-start) | copy-done | bytes 1816
  0.7 1.8 %multiply_convert_fusion.right_ref = bf16[448,256]{1,0:T(8,128)(2,1)} fusion(bf16[448,256]{1,0:T(8,128)(2,1)} %param.4, f32[448]{0:T(512)S(1)} %rsqrt.3), kind=kLoop, calls=%fused_computation | loop fusion | flops 344064 | bytes 460544 | tf_op jit(solution)/shard_map/convert_element_type | solution.py:300
  2.4 47.6 %shard_map.46 = f32[448,256]{1,0:T(8,128)} custom-call(bf16[448,256]{1,0:T(8,128)(2,1)} %multiply_convert_fusion.right_ref, bf16[448,256]{1,0:T(8,128)(2,1)} %sketch_ref.1, f32[1,448]{1,0:T(1,128)} %bitcast.2, f32[1,256]{1,0:T(1,128)} %bitcast.3), custom_call_target="tpu_custom_call" | custom-call | tf_op jit(solution)/shard_map/pallas_call | solution.py:303
  50.0 1.8 %copy.6 = f32[448,256]{1,0:T(8,128)} copy(f32[448,256]{1,0:T(8,128)} %shard_map.46) | data formatting | bytes 917504
  (1 shorter events, 0.0 us)
Async XLA Ops:
  0.0 0.7 %copy-start = (f32[448]{0:T(512)S(1)}, f32[448]{0:T(512)}, u32[]{:S(2)}) copy-start(f32[448]{0:T(512)} %param.6) | copy-start | bytes 5380
